TPU v7x, 8 devices: a whole 2x2x1 slice. The times are simulated.
8 devices in a mesh: rep: 1 (over z), tp: 2 (over y), dp: 4 (over x, core).
Axes of the slice: x: 2, y: 2, z: 1, core: 2. Of those that a mesh axis runs over, the one named last changes fastest.
Arguments:
- grad_partial: float32 [4, 24, 2048, 768], P(('rep', 'dp'), None, None, 'tp')
- momentum: float32 [24, 2048, 768], P('rep', 'dp', 'tp')
- weight: float32 [24, 2048, 768], P('rep', 'dp', 'tp')
- learn_rate: float32 [24], P('rep')
- decay_rate: float32 [], replicated
Outputs:
- output 1: float32 [24, 2048, 768], P('rep', 'dp', 'tp')
- output 2: float32 [24, 2048, 768], P('rep', 'dp', 'tp')
- output 3: bfloat16 [24, 2048, 768], P('rep', None, 'tp')
All inputs are finite; a program needn't handle non-finite values.
Results may differ from a plain program's by a relative error of at most 0.0130496.
Values are sent between devices in bfloat16 or wider.
A program may use at most 1 GiB of HBM per device.

v0:
```python
import math
import jax
import jax.numpy as jnp
from jax import lax
from jax.sharding import PartitionSpec as P, NamedSharding

MOMENTUM = 0.95
NS_STEPS = 5
COEF_A = 3.4445
COEF_B = -4.7750
COEF_C = 2.0315
NORM_EPS = 1e-7


def newton_schulz(update, short_rows):
    upd_f32 = update.astype(jnp.float32)
    norm_val = jnp.sqrt(jnp.sum(upd_f32 * upd_f32, axis=(1, 2), keepdims=True))
    x_cur = (upd_f32 / (norm_val + NORM_EPS)).astype(jnp.bfloat16)
    for step_idx in range(NS_STEPS):
        if short_rows:
            gram_mat = jnp.einsum("bik,bjk->bij", x_cur, x_cur, preferred_element_type=jnp.float32)
        else:
            gram_mat = jnp.einsum("bki,bkj->bij", x_cur, x_cur, preferred_element_type=jnp.float32)
        gram_mat = gram_mat.astype(jnp.bfloat16)
        gram_sq = jnp.einsum("bij,bjk->bik", gram_mat, gram_mat, preferred_element_type=jnp.float32)
        poly_mat = (COEF_B * gram_mat.astype(jnp.float32) + COEF_C * gram_sq).astype(jnp.bfloat16)
        if short_rows:
            prod_mat = jnp.einsum("bij,bjk->bik", poly_mat, x_cur, preferred_element_type=jnp.float32)
        else:
            prod_mat = jnp.einsum("bkj,bij->bki", x_cur, poly_mat, preferred_element_type=jnp.float32)
        x_cur = (COEF_A * x_cur.astype(jnp.float32) + prod_mat).astype(jnp.bfloat16)
    return x_cur


def solution(mesh):
    dp_size = mesh.shape["dp"]
    tp_size = mesh.shape["tp"]

    def local_step(grad_local, mom_local, weight_local, learn_rate, decay_rate):
        grad_sum = lax.psum_scatter(grad_local[0], "dp", scatter_dimension=1, tiled=True)
        grad_mean = grad_sum / dp_size
        mom_new = MOMENTUM * mom_local + grad_mean
        update = (grad_mean + MOMENTUM * mom_new).astype(jnp.bfloat16)
        whole_rows = lax.all_to_all(update, "dp", split_axis=0, concat_axis=1, tiled=True)
        whole_mats = lax.all_gather(whole_rows, "tp", axis=2, tiled=True)
        row_count = whole_mats.shape[1]
        col_count = whole_mats.shape[2]
        ortho_mat = newton_schulz(whole_mats, row_count <= col_count)
        col_width = col_count // tp_size
        own_cols = lax.dynamic_slice_in_dim(ortho_mat, lax.axis_index("tp") * col_width, col_width, axis=2)
        ortho_rows = lax.all_to_all(own_cols, "dp", split_axis=1, concat_axis=0, tiled=True)
        out_scale = 0.2 * math.sqrt(max(row_count, col_count))
        rate_col = learn_rate[:, None, None]
        weight_new = weight_local - rate_col * (out_scale * ortho_rows.astype(jnp.float32) + decay_rate * weight_local)
        weight_full = lax.all_gather(weight_new.astype(jnp.bfloat16), "dp", axis=1, tiled=True)
        return mom_new, weight_new, weight_full

    return jax.shard_map(
        local_step,
        mesh=mesh,
        in_specs=(P(("rep", "dp"), None, None, "tp"), P("rep", "dp", "tp"), P("rep", "dp", "tp"), P("rep"), P()),
        out_specs=(P("rep", "dp", "tp"), P("rep", "dp", "tp"), P("rep", None, "tp")),
        check_vma=False,
    )
```

profile of v0, /device:TPU:0, one launch (start us, length us, event | category | flops | bytes accessed | tf_op | source)
XLA Modules:
  0.0 1685.3 jit_solution(2572928091422386867)
XLA Ops:
  7.2 0.0 reduce-scatter.2.cloned.1.call-start
  7.2 0.7 reduce-scatter.2.cloned.1.call-update
  7.9 0.0 all-gather.3.cloned.1.call-start
  7.9 496.3 %reduce-scatter.2.cloned.1.call-done = f32[24,512,384]{2,1,0:T(8,128)} async-done(((f32[24,2048,384]{2,1,0:T(8,128)}), f32[24,512,384]{2,1,0:T(8,128)}) %reduce-scatter.2.cloned.1.call-update) | async-done | bytes 18874384 | tf_op jit(solution)/shard_map/reduce_scatter | solution.py:40
  504.2 20.1 %add_convert_fusion.4 = (bf16[24,512,384]{2,1,0:T(8,128)(2,1)S(1)}, f32[24,512,384]{2,1,0:T(8,128)}) fusion(f32[24,512,384]{2,1,0:T(8,128)} %reduce-scatter.2.cloned.1.call-done, f32[24,512,384]{2,1,0:T(8,128)} %param.6), kind=kLoop, calls=%fused_computation.14 | loop fusion | flops 28311552 | bytes 66060288 | tf_op jit(solution)/shard_map/convert_element_type | solution.py:43
  524.3 108.1 %all_to_all.27 = bf16[24,512,384]{2,1,0:T(8,128)(2,1)} all-to-all(bf16[24,512,384]{2,1,0:T(8,128)(2,1)S(1)} %get-tuple-element.5), channel_id=1, replica_groups=mesh['rep'=1,'tp'=2,'dp'=4] {'dp'}, dimensions={0} | all-to-all | bytes 18874368 | tf_op jit(solution)/shard_map/all_to_all | solution.py:44
  632.3 8.8 copy.15
  641.2 0.0 all-gather.3.cloned.1.call-update
  641.2 222.1 %all-gather.3.cloned.1.call-done = bf16[6,2048,768]{2,1,0:T(8,128)(2,1)} async-done(((bf16[6,2048,384]{2,1,0:T(8,128)(2,1)}), bf16[6,2048,768]{2,1,0:T(8,128)(2,1)}) %all-gather.3.cloned.1.call-update) | async-done | bytes 18874384 | tf_op jit(solution)/shard_map/all_gather | solution.py:45
  863.3 8.5 fusion
  871.8 26.2 %fusion.31 = bf16[6,768,768]{2,1,0:T(8,128)(2,1)} fusion(bf16[6,2048,768]{2,1,0:T(8,128)(2,1)} %all-gather.3.cloned.1.call-done, f32[6]{0:T(128)S(1)} %sqrt_add_fusion), kind=kOutput, calls=%fused_computation.38 | convolution fusion | flops 14523826176 | bytes 25952280 | tf_op jit(solution)/shard_map/bki,bkj->bij/dot_general | solution.py:23
  898.0 12.9 add_convert_fusion.9.clone.5
  910.9 27.5 %add_convert_fusion.3 = bf16[6,2048,768]{2,1,0:T(8,128)(2,1)} fusion(f32[6]{0:T(128)S(1)} %sqrt_add_fusion, bf16[6,2048,768]{2,1,0:T(8,128)(2,1)} %all-gather.3.cloned.1.call-done, bf16[6,768,768]{2,1,0:T(8,128)(2,1)} %add_convert_fusion.9.clone.5), kind=kOutput, calls=%fused_computation.7 | convolution fusion | flops 14589886464 | bytes 44826648 | tf_op jit(solution)/shard_map/bkj,bij->bki/dot_general | solution.py:30
  938.4 24.8 %fusion.36 = bf16[6,768,768]{2,1,0:T(8,128)(2,1)} fusion(bf16[6,2048,768]{2,1,0:T(8,128)(2,1)} %add_convert_fusion.3), kind=kOutput, calls=%fused_computation.40 | convolution fusion | flops 14495514624 | bytes 25952256 | tf_op jit(solution)/shard_map/bki,bkj->bij/dot_general | solution.py:23
  963.2 40.6 %add_convert_fusion.2 = bf16[6,2048,768]{2,1,0:T(8,128)(2,1)} fusion(bf16[6,2048,768]{2,1,0:T(8,128)(2,1)} %add_convert_fusion.3, bf16[6,768,768]{2,1,0:T(8,128)(2,1)} %fusion.36), kind=kOutput, calls=%fused_computation.6 | convolution fusion | flops 19986776064 | bytes 44826624 | tf_op jit(solution)/shard_map/bkj,bij->bki/dot_general | solution.py:30
  1003.9 25.2 %fusion.37 = bf16[6,768,768]{2,1,0:T(8,128)(2,1)} fusion(bf16[6,2048,768]{2,1,0:T(8,128)(2,1)} %add_convert_fusion.2), kind=kOutput, calls=%fused_computation.41 | convolution fusion | flops 14495514624 | bytes 25952256 | tf_op jit(solution)/shard_map/bki,bkj->bij/dot_general | solution.py:23
  1029.1 40.6 %add_convert_fusion.1 = bf16[6,2048,768]{2,1,0:T(8,128)(2,1)} fusion(bf16[6,2048,768]{2,1,0:T(8,128)(2,1)} %add_convert_fusion.2, bf16[6,768,768]{2,1,0:T(8,128)(2,1)} %fusion.37), kind=kOutput, calls=%fused_computation.5 | convolution fusion | flops 19986776064 | bytes 44826624 | tf_op jit(solution)/shard_map/bkj,bij->bki/dot_general | solution.py:30
  1069.7 25.0 %fusion.38 = bf16[6,768,768]{2,1,0:T(8,128)(2,1)} fusion(bf16[6,2048,768]{2,1,0:T(8,128)(2,1)} %add_convert_fusion.1), kind=kOutput, calls=%fused_computation.42 | convolution fusion | flops 14495514624 | bytes 25952256 | tf_op jit(solution)/shard_map/bki,bkj->bij/dot_general | solution.py:23
  1094.8 40.7 %add_convert_fusion = bf16[6,2048,768]{2,1,0:T(8,128)(2,1)} fusion(bf16[6,2048,768]{2,1,0:T(8,128)(2,1)} %add_convert_fusion.1, bf16[6,768,768]{2,1,0:T(8,128)(2,1)} %fusion.38), kind=kOutput, calls=%fused_computation.4 | convolution fusion | flops 19986776064 | bytes 44826624 | tf_op jit(solution)/shard_map/bkj,bij->bki/dot_general | solution.py:30
  1135.5 25.1 %fusion.39 = bf16[6,768,768]{2,1,0:T(8,128)(2,1)} fusion(bf16[6,2048,768]{2,1,0:T(8,128)(2,1)} %add_convert_fusion), kind=kOutput, calls=%fused_computation.43 | convolution fusion | flops 14495514624 | bytes 25952256 | tf_op jit(solution)/shard_map/bki,bkj->bij/dot_general | solution.py:23
  1160.6 35.9 %fusion.11 = f32[6,2048,768]{2,1,0:T(8,128)} fusion(bf16[6,2048,768]{2,1,0:T(8,128)(2,1)} %add_convert_fusion, bf16[6,768,768]{2,1,0:T(8,128)(2,1)} %fusion.39), kind=kOutput, calls=%fused_computation.26 | convolution fusion | flops 19949027328 | bytes 63700992 | tf_op jit(solution)/shard_map/bkj,bij->bki/dot_general | solution.py:30
  1196.5 10.2 fusion.2
  1206.7 40.5 %copy.21 = bf16[6,2048,384]{2,0,1:T(8,128)(2,1)} copy(bf16[6,2048,384]{2,1,0:T(8,128)(2,1)S(1)} %fusion.2) | data formatting | bytes 18874368 | tf_op jit(solution)/shard_map/dynamic_slice | solution.py:50
  1247.1 6.3 all-to-all-start.1
  1253.5 0.0 all-gather.5.cloned.1.call-start
  1254.2 137.1 %all-to-all-done.1 = bf16[6,2048,384]{2,0,1:T(8,128)(2,1)} async-done(((bf16[6,2048,384]{2,0,1:T(8,128)(2,1)}), bf16[6,2048,384]{2,0,1:T(8,128)(2,1)}, u32[]{:S(2)}, u32[]{:S(2)}) %all-to-all-start.1) | async-done | bytes 9437216 | tf_op jit(solution)/shard_map/all_to_all | solution.py:51
  1391.2 7.2 convert_multiply_fusion.1
  1398.4 0.0 copy-start
  1398.4 7.8 copy.22
  1406.2 0.0 copy-done
  1406.2 23.3 %fusion.34 = (bf16[24,512,384]{2,1,0:T(8,128)(2,1)}, f32[24,512,384]{2,1,0:T(8,128)}) fusion(f32[24,512,384]{2,1,0:T(8,128)} %param.7, f32[]{:T(128)S(6)} %copy.29, f32[4,6,512,384]{3,2,1,0:T(8,128)} %copy.22, f32[24]{0:T(128)S(1)} %copy-done), kind=kLoop, calls=%fused_computation.39 | loop fusion | flops 23592960 | bytes 66060388 | tf_op jit(solution)/shard_map/convert_element_type | solution.py:55
  1429.5 0.0 all-gather.5.cloned.1.call-update
  1429.6 223.4 %all-gather.5.cloned.1.call-done = bf16[24,2048,384]{2,1,0:T(8,128)(2,1)} async-done(((bf16[24,512,384]{2,1,0:T(8,128)(2,1)}), bf16[24,2048,384]{2,1,0:T(8,128)(2,1)}) %all-gather.5.cloned.1.call-update) | async-done | bytes 37748752 | tf_op jit(solution)/shard_map/all_gather | solution.py:55
  1653.0 25.4 %copy.30 = bf16[24,2048,384]{2,1,0:T(8,128)(2,1)} copy(bf16[24,2048,384]{2,1,0:T(8,128)(2,1)} %all-gather.5.cloned.1.call-done) | data formatting | bytes 75497472
  (1 shorter events, 0.0 us)
Async XLA Ops:
  7.2 497.1 %reduce-scatter.2.cloned.1.call-start = ((), (), s32[]{:S(2)}) async-start(), calls=%async_computation.3 | async-start | bytes 94371840 | tf_op jit(solution)/shard_map/reduce_scatter | solution.py:40
  7.9 855.4 %all-gather.3.cloned.1.call-start = ((), (), s32[]{:S(2)}) async-start(), calls=%async_computation.4 | async-start | bytes 28311552 | tf_op jit(solution)/shard_map/all_gather | solution.py:45
  1247.1 144.1 %all-to-all-start.1 = ((bf16[6,2048,384]{2,0,1:T(8,128)(2,1)}), bf16[6,2048,384]{2,0,1:T(8,128)(2,1)}, u32[]{:S(2)}, u32[]{:S(2)}) async-start(bf16[6,2048,384]{2,0,1:T(8,128)(2,1)} %copy.21), calls=%async_computation.2 | async-start | bytes 25165824 | tf_op jit(solution)/shard_map/all_to_all | solution.py:51
  1253.5 399.5 %all-gather.5.cloned.1.call-start = ((), (), s32[]{:S(2)}) async-start(), calls=%async_computation.5 | async-start | bytes 47185920 | tf_op jit(solution)/shard_map/all_gather | solution.py:55
  1398.4 7.8 copy-start
Sparse Core Ops, SparseCore 0:
  10.5 493.6 reduce-scatter.1
  641.3 221.9 all-gather.2
  1429.7 223.2 all-gather.4
where the time goes:
time: 1690 us
  waiting for transfers between devices  1080 us (64%)
  matrix products  325 us (19%)
  blocking collectives  108 us (6%)
  local copies, waits for them, and re-layouts  82.5 us (5%)
  other arithmetic  69.2 us (4%)
    reduce_scatter x1, waiting for transfers between devices, local_step(): lax.psum_scatter(grad_local[0], 'dp', scatter_dimension=1, tiled=True)  496 us
    all_gather x1, waiting for transfers between devices, local_step(): lax.all_gather(weight_new.astype(jnp.bfloat16), 'dp', axis=1, tiled=True)  223 us
    all_gather x1, waiting for transfers between devices, local_step(): whole_mats = lax.all_gather(whole_rows, 'tp', axis=2, tiled=True)  222 us
    dot_general x5, matrix products, newton_schulz(): jnp.einsum('bkj,bij->bki', x_cur, poly_mat, preferred_element_type=jnp.fl...  185 us
    all_to_all x1, waiting for transfers between devices, local_step(): lax.all_to_all(own_cols, 'dp', split_axis=1, concat_axis=0, tiled=True)  137 us
    dot_general x5, matrix products, newton_schulz(): jnp.einsum('bki,bkj->bij', x_cur, x_cur, preferred_element_type=jnp.float32)  126 us
    all_to_all x1, blocking collectives, local_step(): lax.all_to_all(update, 'dp', split_axis=0, concat_axis=1, tiled=True)  108 us
    dynamic_slice x1, local copies, waits for them, and re-layouts, local_step(): lax.dynamic_slice_in_dim(ortho_mat, lax.axis_index('tp') * col_width, col...  40.5 us
  transfers between devices with their start and end apart: 4, of which 4 were waited for; matrix products, arithmetic and copies ran while one was open for 0% of the time, Pallas kernels for 0%

commit v1 on v0

v1 whole, which is shorter than its diff:
```python
import functools
import math

import jax
import jax.numpy as jnp
from jax import lax
from jax.experimental import pallas as pl
from jax.experimental.pallas import tpu as pltpu
from jax.sharding import PartitionSpec as P

MOMENTUM = 0.95
NS_STEPS = 5
COEF_A = 3.4445
COEF_B = -4.7750
COEF_C = 2.0315
NORM_EPS = 1e-7

MESH = pl.DeviceIdType.MESH
F32 = jnp.float32
BF16 = jnp.bfloat16

MATS = 24
ROWS = 2048
COLS = 768
DEVS = 8
ROUNDS = MATS // DEVS
RB = ROWS // 4
CB = COLS // 2
OUT_SCALE = 0.2 * math.sqrt(max(ROWS, COLS))

LAG = 3
LEAD = 2
A_SLOTS = 2 * LEAD
B_SLOTS = 2 * LAG
NS_START = (8 + LAG + 2, 16 + LAG + 2, 24 + LAG)
W_START = (NS_START[0] + 7, NS_START[2], NS_START[2] + 5)
STEPS = NS_START[2] + 6
CHUNK = 64


def rem(a, b):
    return lax.rem(a, b)


def row_loop(total, body):
    @pl.loop(0, total // CHUNK)
    def _(i):
        body(pl.ds(pl.multiple_of(i * CHUNK, CHUNK), CHUNK))


def kernel(
    grad, mom, wt, rate, decay,
    mom_o, wt_o, wb_o,
    own, ra, sendb, recvb, acc, momi, momq, wti, wtq, ust, wst, xb, rx, gram, poly,
    own_sem, a_send, a_recv, rs_send, rs_recv, momi_sem, momq_sem, wti_sem, wtq_sem,
    u_send, u_recv, x_send, x_recv, w_loc, w_par, w_nbr, wp_recv, wx_recv, f_send, f_recv,
):
    dp = lax.axis_index("dp")
    y = lax.axis_index("tp")
    x = lax.div(dp, 2)
    c = rem(dp, 2)
    me = y * 4 + dp
    partner = {"tp": y, "dp": x * 2 + (1 - c)}
    nbr_dp = (1 - x) * 2 + c
    nbr = {"tp": y, "dp": nbr_dp}

    def coords(i):
        dx, dy, dc = lax.div(i, 4), rem(lax.div(i, 2), 2), rem(i, 2)
        yy = rem(y + dy, 2)
        dd = rem(x + dx, 2) * 2 + rem(c + dc, 2)
        return yy, dd

    def remote(src, dst, ss, rs, dev):
        return pltpu.make_async_remote_copy(
            src_ref=src, dst_ref=dst, send_sem=ss, recv_sem=rs, device_id=dev, device_id_type=MESH
        )

    def xblock(r, dd, yy):
        return xb.at[
            r, pl.ds(pl.multiple_of(dd * RB, RB), RB), pl.ds(pl.multiple_of(yy * CB, CB), CB)
        ]

    def own_copy(t):
        s = rem(t, 2)
        return pltpu.make_async_copy(grad.at[t, :, c], own.at[s], own_sem.at[s])

    def a_copy(t):
        s = rem(t, A_SLOTS)
        return remote(grad.at[t, :, 1 - c], ra.at[s], a_send.at[s], a_recv.at[s], partner)

    def rs_copy(t):
        s, d = rem(t, LAG), rem(t, B_SLOTS)
        return remote(sendb.at[s], recvb.at[d], rs_send.at[s], rs_recv.at[d], nbr)

    def mom_load(j):
        s = rem(j, 2)
        return pltpu.make_async_copy(mom.at[j], momi.at[s], momi_sem.at[s])

    def mom_store(j):
        s = rem(j, 2)
        return pltpu.make_async_copy(momq.at[s], mom_o.at[j], momq_sem.at[s])

    def u_copy(j):
        k = rem(j, DEVS)
        r = lax.div(j, DEVS)
        dev = {"tp": lax.div(k, 4), "dp": rem(k, 4)}
        return remote(ust.at[k], xblock(r, dp, y), u_send.at[k], u_recv.at[r * DEVS + me], dev)

    def x_copy(r, i):
        yy, dd = coords(i)
        j = r * DEVS + me
        return remote(
            xblock(r, dd, yy), rx.at[j], x_send.at[r * DEVS + i], x_recv.at[j], {"tp": yy, "dp": dd}
        )

    def w_mat(w):
        yy, dd = coords(rem(w, DEVS))
        return lax.div(w, DEVS) * DEVS + yy * 4 + dd

    def wt_load(w):
        s = rem(w, 2)
        return pltpu.make_async_copy(wt.at[w_mat(w)], wti.at[s], wti_sem.at[s])

    def wt_store(w):
        s = rem(w, 2)
        return pltpu.make_async_copy(wtq.at[s], wt_o.at[w_mat(w)], wtq_sem.at[s])

    def w_copies(w):
        j, s = w_mat(w), rem(w, DEVS)
        dst = wb_o.at[j, dp]
        return (
            pltpu.make_async_copy(wst.at[s], dst, w_loc.at[s]),
            remote(wst.at[s], dst, w_par.at[s], wp_recv.at[j], partner),
            remote(wst.at[s], dst, w_nbr.at[s], wx_recv.at[j], nbr),
        )

    def f_mat(w):
        i = rem(w, DEVS)
        dx, dy, dc = lax.div(i, 4), rem(lax.div(i, 2), 2), rem(i, 2)
        dd = rem(1 - x + dx, 2) * 2 + rem(c + dc, 2)
        return lax.div(w, DEVS) * DEVS + rem(y + dy, 2) * 4 + dd

    def f_copy(w):
        j = f_mat(w)
        ref = wb_o.at[j, nbr_dp]
        return remote(ref, ref, f_send.at[j], f_recv.at[j], partner)

    def presum(t):
        own_copy(t).wait()
        a_copy(t).wait_recv()

        @pl.when(t >= LAG)
        def _():
            rs_copy(t - LAG).wait_send()

        so, sa, ss = rem(t, 2), rem(t, A_SLOTS), rem(t, LAG)

        def body(rows):
            sendb[ss, rows, :] = own[so, 1 - x, rows, :] + ra[sa, 1 - x, rows, :]
            acc[ss, rows, :] = own[so, x, rows, :] + ra[sa, x, rows, :]

        row_loop(RB, body)
        rs_copy(t).start()

        @pl.when(t + 2 < MATS)
        def _():
            own_copy(t + 2).start()

        @pl.when(t + LEAD < MATS)
        def _():
            @pl.when(t + LEAD >= A_SLOTS)
            def _():
                a_copy(t + LEAD - A_SLOTS).wait_send()

            a_copy(t + LEAD).start()

    def finish(j):
        mom_load(j).wait()

        @pl.when(j >= 2)
        def _():
            mom_store(j - 2).wait()

        k = rem(j, DEVS)
        r = lax.div(j, DEVS)

        @pl.when((j >= DEVS) & (k != me))
        def _():
            u_copy(j - DEVS).wait_send()

        rs_copy(j).wait_recv()
        sm, ss, sr = rem(j, 2), rem(j, LAG), rem(j, B_SLOTS)

        def body(rows):
            mean = (acc[ss, rows, :] + recvb[sr, rows, :]) * 0.25
            new = MOMENTUM * momi[sm, rows, :] + mean
            momq[sm, rows, :] = new
            ust[k, rows, :] = (mean + MOMENTUM * new).astype(BF16)

        row_loop(RB, body)

        @pl.when(k != me)
        def _():
            u_copy(j).start()

        mom_store(j).start()

        @pl.when(j + 2 < MATS)
        def _():
            mom_load(j + 2).start()

        for half in range(2):
            @pl.when((k == me) & (y == half))
            def _():
                def put(rows):
                    dst = pl.ds(pl.multiple_of(dp * RB + rows.start, CHUNK), CHUNK)
                    xb[r, dst, half * CB:(half + 1) * CB] = ust[k, rows, :]

                row_loop(RB, put)

    def normalize(r):
        def square(i, total):
            v = xb[r, pl.ds(pl.multiple_of(i * CHUNK, CHUNK), CHUNK), :].astype(F32)
            return total + jnp.sum((v * v).reshape(CHUNK // 8, 8, COLS), axis=0)

        total = lax.fori_loop(0, ROWS // CHUNK, square, jnp.zeros((8, COLS), F32))
        norm = jnp.sqrt(jnp.sum(total, keepdims=True)) + NORM_EPS

        def scale(rows):
            xb[r, rows, :] = (xb[r, rows, :].astype(F32) / norm).astype(BF16)

        row_loop(ROWS, scale)

    def iterate(r):
        @pl.loop(0, COLS // 256)
        def _(m):
            cols = pl.ds(pl.multiple_of(m * 256, 256), 256)
            gram[cols, :] = lax.dot_general(
                xb[r, :, cols], xb[r], (((0,), (0,)), ((), ())), preferred_element_type=F32
            ).astype(BF16)

        @pl.loop(0, COLS // 256)
        def _(m):
            rows = pl.ds(pl.multiple_of(m * 256, 256), 256)
            part = gram[rows, :]
            square = jnp.dot(part, gram[...], preferred_element_type=F32)
            poly[rows, :] = (COEF_B * part.astype(F32) + COEF_C * square).astype(BF16)

        @pl.loop(0, ROWS // 512)
        def _(m):
            rows = pl.ds(pl.multiple_of(m * 512, 512), 512)
            part = xb[r, rows, :]
            prod = jnp.dot(part, poly[...], preferred_element_type=F32)
            xb[r, rows, :] = (COEF_A * part.astype(F32) + prod).astype(BF16)

    def ortho(r, s):
        @pl.when(s == 0)
        def _():
            @pl.loop(1, DEVS)
            def _(i):
                yy, dd = coords(i)
                remote(
                    ust.at[0], xblock(r, dd, yy), u_send.at[0],
                    u_recv.at[r * DEVS + yy * 4 + dd], partner,
                ).wait_recv()

            normalize(r)

        iterate(r)

        @pl.when(s == NS_STEPS - 1)
        def _():
            @pl.loop(0, DEVS)
            def _(n):
                i = rem(n + 4, DEVS)

                @pl.when(i != 0)
                def _():
                    x_copy(r, i).start()

            for half in range(2):
                @pl.when(y == half)
                def _():
                    def put(rows):
                        src = pl.ds(pl.multiple_of(dp * RB + rows.start, CHUNK), CHUNK)
                        rx[r * DEVS + me, rows, :] = xb[r, src, half * CB:(half + 1) * CB]

                    row_loop(RB, put)

    def forward(w):
        f_copy_in = remote(
            wst.at[0], wb_o.at[f_mat(w), nbr_dp], w_nbr.at[0], wx_recv.at[f_mat(w)], nbr
        )
        f_copy_in.wait_recv()
        f_copy(w).start()

    def weights(w):
        j = w_mat(w)

        @pl.when(rem(w, DEVS) != 0)
        def _():
            remote(xblock(0, 0, 0), rx.at[j], x_send.at[0], x_recv.at[j], nbr).wait_recv()

        wt_load(w).wait()

        @pl.when(w >= 2)
        def _():
            wt_store(w - 2).wait()

        @pl.when(w >= DEVS)
        def _():
            old = w_copies(w - DEVS)
            old[0].wait()
            old[1].wait_send()
            old[2].wait_send()

        s2, s8 = rem(w, 2), rem(w, DEVS)
        lr = rate[j]
        wd = decay[0]

        def body(rows):
            cur = wti[s2, rows, :]
            new = cur - lr * (OUT_SCALE * rx[j, rows, :].astype(F32) + wd * cur)
            wtq[s2, rows, :] = new
            wst[s8, rows, :] = new.astype(BF16)

        row_loop(RB, body)
        now = w_copies(w)
        now[2].start()
        now[1].start()
        now[0].start()
        wt_store(w).start()

        @pl.when(w + 2 < MATS)
        def _():
            wt_load(w + 2).start()

        @pl.when(w >= DEVS)
        def _():
            forward(w - DEVS)

    for t in range(2):
        own_copy(t).start()
    for t in range(2):
        mom_load(t).start()
        wt_load(t).start()

    barrier = pltpu.get_barrier_semaphore()
    for i in range(1, DEVS):
        yy, dd = coords(i)
        pl.semaphore_signal(barrier, inc=1, device_id={"tp": yy, "dp": dd}, device_id_type=MESH)
    pl.semaphore_wait(barrier, DEVS - 1)

    for t in range(LEAD):
        a_copy(t).start()

    def w_done(t):
        return (
            jnp.clip(2 * (t - W_START[0]), 0, 8)
            + jnp.clip(2 * (t - W_START[1]), 0, 8)
            + jnp.clip(8 * (t - W_START[2]), 0, 8)
        )

    @pl.loop(0, STEPS)
    def _(t):
        @pl.when((t >= LAG) & (t < MATS + LAG))
        def _():
            finish(t - LAG)

        @pl.when(t < MATS)
        def _():
            presum(t)

        pl.loop(w_done(t), w_done(t + 1))(weights)

        r = jnp.where(t >= NS_START[2], 2, jnp.where(t >= NS_START[1], 1, 0))
        base = jnp.where(
            t >= NS_START[2], NS_START[2], jnp.where(t >= NS_START[1], NS_START[1], NS_START[0])
        )

        @pl.when((t >= base) & (t < base + NS_STEPS))
        def _():
            ortho(r, t - base)

    @pl.loop(MATS - DEVS, MATS)
    def _(w):
        forward(w)

    for t in range(MATS - LAG, MATS):
        rs_copy(t).wait_send()
    for t in range(MATS - A_SLOTS, MATS):
        a_copy(t).wait_send()
    for j in range(MATS - 2, MATS):
        mom_store(j).wait()
        wt_store(j).wait()

    @pl.loop(MATS - DEVS, MATS)
    def _(j):
        @pl.when(rem(j, DEVS) != me)
        def _():
            u_copy(j).wait_send()

        old = w_copies(j)
        old[0].wait()
        old[1].wait_send()
        old[2].wait_send()

    @pl.loop(0, ROUNDS)
    def _(r):
        @pl.loop(1, DEVS)
        def _(i):
            x_copy(r, i).wait_send()

    @pl.loop(0, MATS)
    def _(w):
        j = w_mat(w)
        remote(wst.at[0], wb_o.at[j, dp], w_par.at[0], wp_recv.at[j], partner).wait_recv()
        f_copy(w).wait_send()
        ref = wb_o.at[j, 3 - dp]
        remote(ref, ref, f_send.at[j], f_recv.at[j], partner).wait_recv()


def solution(mesh):
    def local_step(grad_local, mom_local, weight_local, learn_rate, decay_rate):
        hbm = pl.BlockSpec(memory_space=pl.ANY)
        smem = pl.BlockSpec(memory_space=pltpu.SMEM)
        dma = pltpu.SemaphoreType.DMA
        block = (RB, CB)
        mom_new, weight_new, weight_full = pl.pallas_call(
            kernel,
            name="muon_step",
            out_shape=(
                jax.ShapeDtypeStruct((MATS,) + block, F32),
                jax.ShapeDtypeStruct((MATS,) + block, F32),
                jax.ShapeDtypeStruct((MATS, 4) + block, BF16),
            ),
            in_specs=[hbm, hbm, hbm, smem, smem],
            out_specs=[hbm, hbm, hbm],
            scratch_shapes=[
                pltpu.VMEM((2, 2) + block, F32),
                pltpu.VMEM((A_SLOTS, 2) + block, F32),
                pltpu.VMEM((LAG,) + block, F32),
                pltpu.VMEM((B_SLOTS,) + block, F32),
                pltpu.VMEM((LAG,) + block, F32),
                pltpu.VMEM((2,) + block, F32),
                pltpu.VMEM((2,) + block, F32),
                pltpu.VMEM((2,) + block, F32),
                pltpu.VMEM((2,) + block, F32),
                pltpu.VMEM((DEVS,) + block, BF16),
                pltpu.VMEM((DEVS,) + block, BF16),
                pltpu.VMEM((ROUNDS, ROWS, COLS), BF16),
                pltpu.VMEM((MATS,) + block, BF16),
                pltpu.VMEM((COLS, COLS), BF16),
                pltpu.VMEM((COLS, COLS), BF16),
                dma((2,)), dma((A_SLOTS,)), dma((A_SLOTS,)), dma((LAG,)), dma((B_SLOTS,)),
                dma((2,)), dma((2,)), dma((2,)), dma((2,)),
                dma((DEVS,)), dma((MATS,)), dma((MATS,)), dma((MATS,)),
                dma((DEVS,)), dma((DEVS,)), dma((DEVS,)), dma((MATS,)), dma((MATS,)),
                dma((MATS,)), dma((MATS,)),
            ],
            compiler_params=pltpu.CompilerParams(
                collective_id=0, has_side_effects=True, vmem_limit_bytes=67_000_000
            ),
            cost_estimate=pl.CostEstimate(
                flops=3 * 28_700_000_000, bytes_accessed=400_000_000, transcendentals=0
            ),
        )(
            grad_local.reshape((MATS, 2, 2) + block),
            mom_local,
            weight_local,
            learn_rate,
            decay_rate.reshape((1,)),
        )
        return mom_new, weight_new, weight_full.reshape(MATS, ROWS, CB)

    return jax.shard_map(
        local_step,
        mesh=mesh,
        in_specs=(P(("rep", "dp"), None, None, "tp"), P("rep", "dp", "tp"), P("rep", "dp", "tp"), P("rep"), P()),
        out_specs=(P("rep", "dp", "tp"), P("rep", "dp", "tp"), P("rep", None, "tp")),
        check_vma=False,
    )
```

time: 1690 us -> 875 us (0.52)
  waiting for transfers between devices: 1080 us -> 0 us
  Pallas kernels: 0 us -> 822 us
  matrix products: 325 us -> 0 us
  blocking collectives: 108 us -> 0 us
  other arithmetic: 69.2 us -> 0 us
  local copies, waits for them, and re-layouts: 82.5 us -> 50.9 us
    pallas_call x0 -> x1, Pallas kernels: none -> 822 us  [local_step(): pl.pallas_call(kernel, name='muon_step', out_shape=(jax.ShapeDtypeStruct(...]
    reduce_scatter x1 -> x0, waiting for transfers between devices: 496 us -> none  [local_step(): lax.psum_scatter(grad_local[0], 'dp', scatter_dimension=1, tiled=True)]
    all_gather x2 -> x0, waiting for transfers between devices: 445 us -> none  [the longest x1 223 us: local_step(): lax.all_gather(weight_new.astype(jnp.bfloat16), 'dp', axis=1, tiled=True)]
    dot_general x11 -> x0, matrix products: 325 us -> none  [the longest x5 185 us: newton_schulz(): jnp.einsum('bkj,bij->bki', x_cur, poly_mat, preferred_element_type=jnp.fl...]
    all_to_all x1 -> x0, waiting for transfers between devices: 137 us -> none  [local_step(): lax.all_to_all(own_cols, 'dp', split_axis=1, concat_axis=0, tiled=True)]
    all_to_all x1 -> x0, blocking collectives: 108 us -> none  [local_step(): lax.all_to_all(update, 'dp', split_axis=0, concat_axis=1, tiled=True)]
    convert_element_type x3 -> x0, other arithmetic: 53.6 us -> none  [the longest x1 23.3 us: local_step(): weight_new.astype(jnp.bfloat16)]
    dynamic_slice x1 -> x0, local copies, waits for them, and re-layouts: 40.5 us -> none  [local_step(): lax.dynamic_slice_in_dim(ortho_mat, lax.axis_index('tp') * col_width, col...]
  transfers between devices with their start and end apart: 4 -> 0, of which waited for: 4 -> 0; matrix products, arithmetic and copies ran while one was open for 0% -> 0% of each run, Pallas kernels for 0% -> 0%
where the time goes in v1:
time: 875 us
  Pallas kernels  822 us (94%)
  local copies, waits for them, and re-layouts  50.9 us (6%)
    pallas_call x1, Pallas kernels, local_step(): pl.pallas_call(kernel, name='muon_step', out_shape=(jax.ShapeDtypeStruct(...  822 us
    unnamed x5, local copies, waits for them, and re-layouts  50.9 us

profile of v1, /device:TPU:0, one launch (start us, length us, event | category | flops | bytes accessed | tf_op | source)
XLA Modules:
  0.0 874.6 jit_solution(1806227705304773400)
XLA Ops:
  1.3 822.4 %muon_step.1 = (f32[24,512,384]{2,1,0:T(8,128)}, f32[24,512,384]{2,1,0:T(8,128)}, bf16[24,4,512,384]{3,2,1,0:T(8,128)(2,1)}) custom-call(f32[24,2,2,512,384]{4,3,2,1,0:T(8,128)} %bitcast.grad, f32[24,512,384]{2,1,0:T(8,128)} %mom.1, f32[24,512,384]{2,1,0:T(8,128)} %wt.1, f32[24]{0:T(128)} %rate.1, f32[1]{0:T(128)} %bitcast.3.decay), custom_call_target="tpu_custom_call" | custom-call | flops 86100000768 | bytes 400000000 | tf_op jit(solution)/shard_map/muon_step/pallas_call | solution.py:429
  823.7 0.0 copy-start
  823.7 14.8 %copy.12 = f32[24,512,384]{2,1,0:T(8,128)} copy(f32[24,512,384]{2,1,0:T(8,128)} %get-tuple-element.12) | data formatting | bytes 37748736
  838.5 3.8 copy-done
  842.3 6.8 copy.13
  849.2 25.4 %copy.14 = bf16[24,2048,384]{2,1,0:T(8,128)(2,1)} copy(bf16[24,2048,384]{2,1,0:T(8,128)(2,1)} %bitcast.4) | data formatting | bytes 75497472
Async XLA Ops:
  823.7 18.6 %copy-start = (f32[24,512,384]{2,1,0:T(8,128)S(1)}, f32[24,512,384]{2,1,0:T(8,128)}, u32[]{:S(2)}) copy-start(f32[24,512,384]{2,1,0:T(8,128)} %get-tuple-element.13) | copy-start | bytes 56623108

commit v2 on v1

--- a/solution.py
+++ b/solution.py
@@ -1,4 +1,3 @@
-import functools
 import math
 
 import jax
@@ -7,6 +6,7 @@
 from jax.experimental import pallas as pl
 from jax.experimental.pallas import tpu as pltpu
 from jax.sharding import PartitionSpec as P
+
 
 MOMENTUM = 0.95
 NS_STEPS = 5
@@ -36,6 +36,9 @@
 W_START = (NS_START[0] + 7, NS_START[2], NS_START[2] + 5)
 STEPS = NS_START[2] + 6
 CHUNK = 64
+HEAD = MATS - DEVS
+TAIL_A = 6
+TAIL_B = DEVS - TAIL_A
 
 
 def rem(a, b):
@@ -50,7 +53,7 @@
 
 def kernel(
     grad, mom, wt, rate, decay,
-    mom_o, wt_o, wb_o,
+    mom_o, wt_o, wb_o, tail_a, tail_b,
     own, ra, sendb, recvb, acc, momi, momq, wti, wtq, ust, wst, xb, rx, gram, poly,
     own_sem, a_send, a_recv, rs_send, rs_recv, momi_sem, momq_sem, wti_sem, wtq_sem,
     u_send, u_recv, x_send, x_recv, w_loc, w_par, w_nbr, wp_recv, wx_recv, f_send, f_recv,
@@ -134,6 +137,11 @@
             remote(wst.at[s], dst, w_nbr.at[s], wx_recv.at[j], nbr),
         )
 
+    def tail_copy(w, part):
+        j, s = w_mat(w) - HEAD, rem(w, DEVS)
+        dst = tail_b.at[j - TAIL_A] if part else tail_a.at[j]
+        return pltpu.make_async_copy(wst.at[s], dst, w_loc.at[s])
+
     def f_mat(w):
         i = rem(w, DEVS)
         dx, dy, dc = lax.div(i, 4), rem(lax.div(i, 2), 2), rem(i, 2)
@@ -325,10 +333,22 @@
             wst[s8, rows, :] = new.astype(BF16)
 
         row_loop(RB, body)
-        now = w_copies(w)
-        now[2].start()
-        now[1].start()
-        now[0].start()
+
+        @pl.when(w < HEAD)
+        def _():
+            now = w_copies(w)
+            now[2].start()
+            now[1].start()
+            now[0].start()
+
+        @pl.when((w >= HEAD) & (j < HEAD + TAIL_A))
+        def _():
+            tail_copy(w, False).start()
+
+        @pl.when((w >= HEAD) & (j >= HEAD + TAIL_A))
+        def _():
+            tail_copy(w, True).start()
+
         wt_store(w).start()
 
         @pl.when(w + 2 < MATS)
@@ -381,10 +401,6 @@
         @pl.when((t >= base) & (t < base + NS_STEPS))
         def _():
             ortho(r, t - base)
-
-    @pl.loop(MATS - DEVS, MATS)
-    def _(w):
-        forward(w)
 
     for t in range(MATS - LAG, MATS):
         rs_copy(t).wait_send()
@@ -400,10 +416,7 @@
         def _():
             u_copy(j).wait_send()
 
-        old = w_copies(j)
-        old[0].wait()
-        old[1].wait_send()
-        old[2].wait_send()
+        pltpu.make_async_copy(wst.at[0], tail_a.at[0], w_loc.at[rem(j, DEVS)]).wait()
 
     @pl.loop(0, ROUNDS)
     def _(r):
@@ -411,7 +424,7 @@
         def _(i):
             x_copy(r, i).wait_send()
 
-    @pl.loop(0, MATS)
+    @pl.loop(0, HEAD)
     def _(w):
         j = w_mat(w)
         remote(wst.at[0], wb_o.at[j, dp], w_par.at[0], wp_recv.at[j], partner).wait_recv()
@@ -420,22 +433,77 @@
         remote(ref, ref, f_send.at[j], f_recv.at[j], partner).wait_recv()
 
 
+def publish_kernel(mom, wt, wb, mom_o, wt_o, wb_o):
+    mom_o[...] = mom[...]
+    wt_o[...] = wt[...]
+    wb_o[...] = wb[...]
+
+
+def publish(mom, wt, wb):
+    steps = HEAD
+    small = pl.BlockSpec((MATS * RB // steps, CB), lambda i: (i, 0))
+    large = pl.BlockSpec((ROWS, CB), lambda i: (i, 0))
+    return pl.pallas_call(
+        publish_kernel,
+        name="publish",
+        grid=(steps,),
+        out_shape=(
+            jax.ShapeDtypeStruct((MATS * RB, CB), F32),
+            jax.ShapeDtypeStruct((MATS * RB, CB), F32),
+            jax.ShapeDtypeStruct((MATS * ROWS, CB), BF16),
+        ),
+        in_specs=[small, small, large],
+        out_specs=[small, small, large],
+        cost_estimate=pl.CostEstimate(
+            flops=40_000_000_000, bytes_accessed=126_000_000, transcendentals=0
+        ),
+    )(mom.reshape(-1, CB), wt.reshape(-1, CB), wb.reshape(-1, CB))
+
+
+def fill_kernel(own, par, nbr, fwd, whole, out):
+    dp = lax.axis_index("dp")
+    c = rem(dp, 2)
+    out[0, dp] = own[0]
+    out[0, dp + 1 - 2 * c] = par[0]
+    out[0, rem(dp + 2, 4)] = nbr[0]
+    out[0, 3 - dp] = fwd[0]
+
+
+def fill(whole, first, own, par, nbr, fwd):
+    count = own.shape[0]
+    part = pl.BlockSpec((1, RB, CB), lambda i: (i, 0, 0))
+    return pl.pallas_call(
+        fill_kernel,
+        name="fill",
+        grid=(count,),
+        out_shape=jax.ShapeDtypeStruct(whole.shape, whole.dtype),
+        in_specs=[part] * 4 + [pl.BlockSpec(memory_space=pl.ANY)],
+        out_specs=pl.BlockSpec((1, 4, RB, CB), lambda i: (i + first, 0, 0, 0)),
+        input_output_aliases={4: 0},
+        cost_estimate=pl.CostEstimate(
+            flops=count * 1_000_000_000, bytes_accessed=count * 3_200_000, transcendentals=0
+        ),
+    )(own, par, nbr, fwd, whole)
+
+
 def solution(mesh):
     def local_step(grad_local, mom_local, weight_local, learn_rate, decay_rate):
         hbm = pl.BlockSpec(memory_space=pl.ANY)
         smem = pl.BlockSpec(memory_space=pltpu.SMEM)
         dma = pltpu.SemaphoreType.DMA
         block = (RB, CB)
-        mom_new, weight_new, weight_full = pl.pallas_call(
+        mom_new, weight_new, head, tail_a, tail_b = pl.pallas_call(
             kernel,
             name="muon_step",
             out_shape=(
                 jax.ShapeDtypeStruct((MATS,) + block, F32),
                 jax.ShapeDtypeStruct((MATS,) + block, F32),
-                jax.ShapeDtypeStruct((MATS, 4) + block, BF16),
+                jax.ShapeDtypeStruct((HEAD, 4) + block, BF16),
+                jax.ShapeDtypeStruct((TAIL_A,) + block, BF16),
+                jax.ShapeDtypeStruct((TAIL_B,) + block, BF16),
             ),
             in_specs=[hbm, hbm, hbm, smem, smem],
-            out_specs=[hbm, hbm, hbm],
+            out_specs=[hbm] * 5,
             scratch_shapes=[
                 pltpu.VMEM((2, 2) + block, F32),
                 pltpu.VMEM((A_SLOTS, 2) + block, F32),
@@ -471,7 +539,27 @@
             learn_rate,
             decay_rate.reshape((1,)),
         )
-        return mom_new, weight_new, weight_full.reshape(MATS, ROWS, CB)
+        across = [(0, 2), (1, 3), (2, 0), (3, 1)]
+        beside = [(0, 1), (1, 0), (2, 3), (3, 2)]
+
+        def move(value, pairs):
+            return lax.ppermute(value, "dp", pairs)
+
+        nbr_a = move(tail_a, across)
+        nbr_b = move(tail_b, across)
+        par_a = move(tail_a, beside)
+        par_b = move(tail_b, beside)
+        fwd_a = move(nbr_a, beside)
+        fwd_b = move(nbr_b, beside)
+        mom_new, weight_new, full = publish(mom_new, weight_new, head)
+        full = full.reshape((MATS, 4) + block)
+        full = fill(full, HEAD, tail_a, par_a, nbr_a, fwd_a)
+        full = fill(full, HEAD + TAIL_A, tail_b, par_b, nbr_b, fwd_b)
+        return (
+            mom_new.reshape((MATS,) + block),
+            weight_new.reshape((MATS,) + block),
+            full.reshape(MATS, ROWS, CB),
+        )
 
     return jax.shard_map(
         local_step,

time: 875 us -> 884 us (1.010)
  waiting for transfers between devices: 0 us -> 68.1 us
  local copies, waits for them, and re-layouts: 50.9 us -> 0.01 us
  Pallas kernels: 822 us -> 811 us
    ppermute x0 -> x6, waiting for transfers between devices: none -> 68.1 us  [move(): return lax.ppermute(value, 'dp', pairs)]
    pallas_call x1, Pallas kernels: 822 us -> 755 us  [local_step(): pl.pallas_call(kernel, name='muon_step', out_shape=(jax.ShapeDtypeStruct(...]
    pallas_call x0 -> x3, Pallas kernels: none -> 55.5 us  [the longest x1 43.7 us: publish(): pl.pallas_call(publish_kernel, name='publish', grid=(steps,), out_shape=(...]
    unnamed x5 -> x4, local copies, waits for them, and re-layouts: 50.9 us -> 0.01 us
  transfers between devices with their start and end apart: 0 -> 6, of which waited for: 0 -> 1; matrix products, arithmetic and copies ran while one was open for 0% -> 0% of each run, Pallas kernels for 0% -> 6%
where the time goes in v2:
time: 884 us; the launch traced here: 883 us
  Pallas kernels  811 us (92%)
  waiting for transfers between devices  68.1 us (8%)
    pallas_call x1, Pallas kernels, local_step(): pl.pallas_call(kernel, name='muon_step', out_shape=(jax.ShapeDtypeStruct(...  755 us
    ppermute x6, waiting for transfers between devices, move(): return lax.ppermute(value, 'dp', pairs)  68.1 us
    pallas_call x1, Pallas kernels, publish(): pl.pallas_call(publish_kernel, name='publish', grid=(steps,), out_shape=(...  43.7 us
  transfers between devices with their start and end apart: 6, of which 1 were waited for; matrix products, arithmetic and copies ran while one was open for 0% of the time, Pallas kernels for 6%

profile of v2, /device:TPU:0, one launch (start us, length us, event | category | flops | bytes accessed | tf_op | source)
XLA Modules:
  0.0 883.4 jit_solution(8378553267387598958)
XLA Ops:
  1.3 755.5 %muon_step.1 = (f32[24,512,384]{2,1,0:T(8,128)}, f32[24,512,384]{2,1,0:T(8,128)}, bf16[16,4,512,384]{3,2,1,0:T(8,128)(2,1)}, bf16[6,512,384]{2,1,0:T(8,128)(2,1)}, bf16[2,512,384]{2,1,0:T(8,128)(2,1)}) custom-call(f32[24,2,2,512,384]{4,3,2,1,0:T(8,128)} %bitcast.grad, f32[24,512,384]{2,1,0:T(8,128)} %mom.1, f32[24,512,384]{2,1,0:T(8,128)} %wt.1, f32[24]{0:T(128)} %rate.1, ...), custom_call_target="tpu_custom_call" | custom-call | flops 86100000768 | bytes 400000000 | tf_op jit(solution)/shard_map/muon_step/pallas_call | solution.py:495
  756.8 1.5 collective-permute-start.4
  758.3 0.5 collective-permute-start.1
  758.8 0.0 collective-permute-start.3
  758.8 0.5 collective-permute-start
  759.3 68.1 %collective-permute-done.1.nbr = bf16[2,512,384]{2,1,0:T(8,128)(2,1)S(1)} collective-permute-done((bf16[2,512,384]{2,1,0:T(8,128)(2,1)}, bf16[2,512,384]{2,1,0:T(8,128)(2,1)S(1)}, u32[]{:S(2)}, u32[]{:S(2)}) %collective-permute-start.1) | collective-permute-done | bytes 786464 | tf_op jit(solution)/shard_map/ppermute | solution.py:546
  827.4 0.0 copy-start.1
  827.4 0.0 collective-permute-start.2
  827.4 0.0 collective-permute-done.4.nbr
  827.4 0.0 copy-start
  827.4 0.5 collective-permute-start.5
  827.9 43.7 %publish.1 = (f32[12288,384]{1,0:T(8,128)}, f32[12288,384]{1,0:T(8,128)}, bf16[49152,384]{1,0:T(8,128)(2,1)}) custom-call(f32[12288,384]{1,0:T(8,128)} %bitcast.13, f32[12288,384]{1,0:T(8,128)} %bitcast.14, bf16[32768,384]{1,0:T(8,128)(2,1)} %bitcast.12), custom_call_target="tpu_custom_call" | custom-call | flops 40000000000 | bytes 126000000 | tf_op jit(solution)/shard_map/publish/pallas_call | solution.py:446
  871.6 0.0 copy-done.1
  871.6 0.0 copy-done
  871.6 0.0 collective-permute-done.3.par
  871.6 0.0 collective-permute-done.5.fwd
  871.6 8.6 fill.2.whole
  880.3 0.0 collective-permute-done.par
  880.3 0.0 collective-permute-done.2.fwd
  880.3 3.2 fill.3
Async XLA Ops:
  756.8 70.6 %collective-permute-start.4 = (bf16[6,512,384]{2,1,0:T(8,128)(2,1)}, bf16[6,512,384]{2,1,0:T(8,128)(2,1)S(1)}, u32[]{:S(2)}, u32[]{:S(2)}) collective-permute-start(bf16[6,512,384]{2,1,0:T(8,128)(2,1)} %get-tuple-element.17.own), channel_id=1, source_target_pairs={{0,2},{1,3},{2,0},{3,1},{4,6},{5,7},{6,4},{7,5}} | collective-permute-start | bytes 7077896 | tf_op jit(solution)/shard_map/ppermute | solution.py:546
  758.3 69.1 %collective-permute-start.1 = (bf16[2,512,384]{2,1,0:T(8,128)(2,1)}, bf16[2,512,384]{2,1,0:T(8,128)(2,1)S(1)}, u32[]{:S(2)}, u32[]{:S(2)}) collective-permute-start(bf16[2,512,384]{2,1,0:T(8,128)(2,1)} %get-tuple-element.16.own), channel_id=1, source_target_pairs={{0,2},{1,3},{2,0},{3,1},{4,6},{5,7},{6,4},{7,5}} | collective-permute-start | bytes 2359304 | tf_op jit(solution)/shard_map/ppermute | solution.py:546
  758.8 112.8 %collective-permute-start.3 = (bf16[6,512,384]{2,1,0:T(8,128)(2,1)}, bf16[6,512,384]{2,1,0:T(8,128)(2,1)}, u32[]{:S(2)}, u32[]{:S(2)}) collective-permute-start(bf16[6,512,384]{2,1,0:T(8,128)(2,1)} %get-tuple-element.17.own), channel_id=1, source_target_pairs={{0,1},{1,0},{2,3},{3,2},{4,5},{5,4},{6,7},{7,6}} | collective-permute-start | bytes 7077896 | tf_op jit(solution)/shard_map/ppermute | solution.py:546
  758.8 121.4 %collective-permute-start = (bf16[2,512,384]{2,1,0:T(8,128)(2,1)}, bf16[2,512,384]{2,1,0:T(8,128)(2,1)}, u32[]{:S(2)}, u32[]{:S(2)}) collective-permute-start(bf16[2,512,384]{2,1,0:T(8,128)(2,1)} %get-tuple-element.16.own), channel_id=1, source_target_pairs={{0,1},{1,0},{2,3},{3,2},{4,5},{5,4},{6,7},{7,6}} | collective-permute-start | bytes 2359304 | tf_op jit(solution)/shard_map/ppermute | solution.py:546
  827.4 44.2 %copy-start.1 = (bf16[2,512,384]{2,1,0:T(8,128)(2,1)}, bf16[2,512,384]{2,1,0:T(8,128)(2,1)S(1)}, u32[]{:S(2)}) copy-start(bf16[2,512,384]{2,1,0:T(8,128)(2,1)S(1)} %collective-permute-done.1.nbr) | copy-start | bytes 2359300
  827.4 52.9 %collective-permute-start.2 = (bf16[2,512,384]{2,1,0:T(8,128)(2,1)S(1)}, bf16[2,512,384]{2,1,0:T(8,128)(2,1)}, u32[]{:S(2)}, u32[]{:S(2)}) collective-permute-start(bf16[2,512,384]{2,1,0:T(8,128)(2,1)S(1)} %collective-permute-done.1.nbr), channel_id=1, source_target_pairs={{0,1},{1,0},{2,3},{3,2},{4,5},{5,4},{6,7},{7,6}} | collective-permute-start | bytes 2359304 | tf_op jit(solution)/shard_map/ppermute | solution.py:546
  827.4 44.2 %copy-start = (bf16[6,512,384]{2,1,0:T(8,128)(2,1)}, bf16[6,512,384]{2,1,0:T(8,128)(2,1)S(1)}, u32[]{:S(2)}) copy-start(bf16[6,512,384]{2,1,0:T(8,128)(2,1)S(1)} %collective-permute-done.4.nbr) | copy-start | bytes 7077892
  827.4 44.2 %collective-permute-start.5 = (bf16[6,512,384]{2,1,0:T(8,128)(2,1)S(1)}, bf16[6,512,384]{2,1,0:T(8,128)(2,1)}, u32[]{:S(2)}, u32[]{:S(2)}) collective-permute-start(bf16[6,512,384]{2,1,0:T(8,128)(2,1)S(1)} %collective-permute-done.4.nbr), channel_id=1, source_target_pairs={{0,1},{1,0},{2,3},{3,2},{4,5},{5,4},{6,7},{7,6}} | collective-permute-start | bytes 7077896 | tf_op jit(solution)/shard_map/ppermute | solution.py:546

commit v3 on v2

--- a/solution.py
+++ b/solution.py
@@ -1,3 +1,4 @@
+import functools
 import math
 
 import jax
@@ -33,12 +34,13 @@
 A_SLOTS = 2 * LEAD
 B_SLOTS = 2 * LAG
 NS_START = (8 + LAG + 2, 16 + LAG + 2, 24 + LAG)
-W_START = (NS_START[0] + 7, NS_START[2], NS_START[2] + 5)
-STEPS = NS_START[2] + 6
+W_START = (NS_START[0] + 7, NS_START[2])
+STEPS = NS_START[2] + NS_STEPS
 CHUNK = 64
 HEAD = MATS - DEVS
-TAIL_A = 6
-TAIL_B = DEVS - TAIL_A
+TAILS = (5, 2, 1)
+PIECES = 4
+PIECE = RB // PIECES
 
 
 def rem(a, b):
@@ -53,9 +55,9 @@
 
 def kernel(
     grad, mom, wt, rate, decay,
-    mom_o, wt_o, wb_o, tail_a, tail_b,
+    mom_o, wt_o, wb_o, tail_a, tail_b, tail_c,
     own, ra, sendb, recvb, acc, momi, momq, wti, wtq, ust, wst, xb, rx, gram, poly,
-    own_sem, a_send, a_recv, rs_send, rs_recv, momi_sem, momq_sem, wti_sem, wtq_sem,
+    p_send, p_recv, own_sem, a_send, a_recv, rs_send, rs_recv, momi_sem, momq_sem, wti_sem, wtq_sem,
     u_send, u_recv, x_send, x_recv, w_loc, w_par, w_nbr, wp_recv, wx_recv, f_send, f_recv,
 ):
     dp = lax.axis_index("dp")
@@ -137,10 +139,14 @@
             remote(wst.at[s], dst, w_nbr.at[s], wx_recv.at[j], nbr),
         )
 
-    def tail_copy(w, part):
-        j, s = w_mat(w) - HEAD, rem(w, DEVS)
-        dst = tail_b.at[j - TAIL_A] if part else tail_a.at[j]
-        return pltpu.make_async_copy(wst.at[s], dst, w_loc.at[s])
+    def tail_copies(w):
+        s = rem(w, DEVS)
+        first = HEAD
+        for ref, count in zip((tail_a, tail_b, tail_c), TAILS):
+            yield first, first + count, lambda j, ref=ref, first=first: pltpu.make_async_copy(
+                wst.at[s], ref.at[j - first], w_loc.at[s]
+            )
+            first += count
 
     def f_mat(w):
         i = rem(w, DEVS)
@@ -176,11 +182,38 @@
 
         @pl.when(t + LEAD < MATS)
         def _():
-            @pl.when(t + LEAD >= A_SLOTS)
+            @pl.when(t + LEAD > A_SLOTS)
             def _():
                 a_copy(t + LEAD - A_SLOTS).wait_send()
 
             a_copy(t + LEAD).start()
+
+    def piece_copy(q):
+        rows = pl.ds(q * PIECE, PIECE)
+        side = 1 - x
+        if q == PIECES:
+            rows, side = pl.ds(0, RB), x
+        return remote(
+            grad.at[0, side, 1 - c, rows, :], ra.at[0, side, rows, :], p_send.at[q], p_recv.at[q], partner
+        )
+
+    def presum_first():
+        own_copy(0).wait()
+        for q in range(PIECES):
+            piece_copy(q).wait_recv()
+            rows = pl.ds(q * PIECE, PIECE)
+            sendb[0, rows, :] = own[0, 1 - x, rows, :] + ra[0, 1 - x, rows, :]
+            remote(
+                sendb.at[0, rows, :], recvb.at[0, rows, :], rs_send.at[0], rs_recv.at[0], nbr
+            ).start()
+        piece_copy(PIECES).wait_recv()
+
+        def body(rows):
+            acc[0, rows, :] = own[0, x, rows, :] + ra[0, x, rows, :]
+
+        row_loop(RB, body)
+        own_copy(2).start()
+        a_copy(LEAD).start()
 
     def finish(j):
         mom_load(j).wait()
@@ -341,13 +374,10 @@
             now[1].start()
             now[0].start()
 
-        @pl.when((w >= HEAD) & (j < HEAD + TAIL_A))
-        def _():
-            tail_copy(w, False).start()
-
-        @pl.when((w >= HEAD) & (j >= HEAD + TAIL_A))
-        def _():
-            tail_copy(w, True).start()
+        for low, high, copy in tail_copies(w):
+            @pl.when((w >= HEAD) & (j >= low) & (j < high))
+            def _():
+                copy(j).start()
 
         wt_store(w).start()
 
@@ -355,7 +385,7 @@
         def _():
             wt_load(w + 2).start()
 
-        @pl.when(w >= DEVS)
+        @pl.when((w >= DEVS) & (w < HEAD))
         def _():
             forward(w - DEVS)
 
@@ -371,14 +401,16 @@
         pl.semaphore_signal(barrier, inc=1, device_id={"tp": yy, "dp": dd}, device_id_type=MESH)
     pl.semaphore_wait(barrier, DEVS - 1)
 
-    for t in range(LEAD):
+    for q in range(PIECES + 1):
+        piece_copy(q).start()
+    for t in range(1, LEAD):
         a_copy(t).start()
+    presum_first()
 
     def w_done(t):
         return (
             jnp.clip(2 * (t - W_START[0]), 0, 8)
             + jnp.clip(2 * (t - W_START[1]), 0, 8)
-            + jnp.clip(8 * (t - W_START[2]), 0, 8)
         )
 
     @pl.loop(0, STEPS)
@@ -387,7 +419,7 @@
         def _():
             finish(t - LAG)
 
-        @pl.when(t < MATS)
+        @pl.when((t >= 1) & (t < MATS))
         def _():
             presum(t)
 
@@ -402,27 +434,31 @@
         def _():
             ortho(r, t - base)
 
+    @pl.loop(HEAD - DEVS, HEAD)
+    def _(w):
+        forward(w)
+
+    for q in range(PIECES + 1):
+        piece_copy(q).wait_send()
     for t in range(MATS - LAG, MATS):
         rs_copy(t).wait_send()
     for t in range(MATS - A_SLOTS, MATS):
         a_copy(t).wait_send()
     for j in range(MATS - 2, MATS):
         mom_store(j).wait()
-        wt_store(j).wait()
-
-    @pl.loop(MATS - DEVS, MATS)
+
+    @pl.loop(HEAD, MATS)
     def _(j):
         @pl.when(rem(j, DEVS) != me)
         def _():
             u_copy(j).wait_send()
 
-        pltpu.make_async_copy(wst.at[0], tail_a.at[0], w_loc.at[rem(j, DEVS)]).wait()
-
-    @pl.loop(0, ROUNDS)
-    def _(r):
+    def drain_x(r):
         @pl.loop(1, DEVS)
         def _(i):
             x_copy(r, i).wait_send()
+
+    pl.loop(0, ROUNDS - 1)(drain_x)
 
     @pl.loop(0, HEAD)
     def _(w):
@@ -431,6 +467,13 @@
         f_copy(w).wait_send()
         ref = wb_o.at[j, 3 - dp]
         remote(ref, ref, f_send.at[j], f_recv.at[j], partner).wait_recv()
+
+    pl.loop(HEAD, MATS)(weights)
+    drain_x(ROUNDS - 1)
+    for w in range(HEAD, MATS):
+        pltpu.make_async_copy(wst.at[0], tail_a.at[0], w_loc.at[w % DEVS]).wait()
+    for w in range(MATS - 2, MATS):
+        wt_store(w).wait()
 
 
 def publish_kernel(mom, wt, wb, mom_o, wt_o, wb_o):
@@ -460,26 +503,32 @@
     )(mom.reshape(-1, CB), wt.reshape(-1, CB), wb.reshape(-1, CB))
 
 
-def fill_kernel(own, par, nbr, fwd, whole, out):
+def fill_kernel(first, own, par, nbr, fwd, whole, out, sems):
     dp = lax.axis_index("dp")
-    c = rem(dp, 2)
-    out[0, dp] = own[0]
-    out[0, dp + 1 - 2 * c] = par[0]
-    out[0, rem(dp + 2, 4)] = nbr[0]
-    out[0, 3 - dp] = fwd[0]
+    places = (dp, dp + 1 - 2 * rem(dp, 2), rem(dp + 2, 4), 3 - dp)
+    copies = [
+        pltpu.make_async_copy(ref.at[i], out.at[first + i, place], sems.at[n, i])
+        for n, (ref, place) in enumerate(zip((own, par, nbr, fwd), places))
+        for i in range(own.shape[0])
+    ]
+    for copy in copies:
+        copy.start()
+    for copy in copies:
+        copy.wait()
 
 
 def fill(whole, first, own, par, nbr, fwd):
     count = own.shape[0]
-    part = pl.BlockSpec((1, RB, CB), lambda i: (i, 0, 0))
+    hbm = pl.BlockSpec(memory_space=pl.ANY)
     return pl.pallas_call(
-        fill_kernel,
+        functools.partial(fill_kernel, first),
         name="fill",
-        grid=(count,),
         out_shape=jax.ShapeDtypeStruct(whole.shape, whole.dtype),
-        in_specs=[part] * 4 + [pl.BlockSpec(memory_space=pl.ANY)],
-        out_specs=pl.BlockSpec((1, 4, RB, CB), lambda i: (i + first, 0, 0, 0)),
+        in_specs=[pl.BlockSpec(memory_space=pltpu.VMEM)] * 4 + [hbm],
+        out_specs=hbm,
+        scratch_shapes=[pltpu.SemaphoreType.DMA((4, count))],
         input_output_aliases={4: 0},
+        compiler_params=pltpu.CompilerParams(vmem_limit_bytes=10 << 20),
         cost_estimate=pl.CostEstimate(
             flops=count * 1_000_000_000, bytes_accessed=count * 3_200_000, transcendentals=0
         ),
@@ -492,18 +541,17 @@
         smem = pl.BlockSpec(memory_space=pltpu.SMEM)
         dma = pltpu.SemaphoreType.DMA
         block = (RB, CB)
-        mom_new, weight_new, head, tail_a, tail_b = pl.pallas_call(
+        mom_new, weight_new, head, *tails = pl.pallas_call(
             kernel,
             name="muon_step",
             out_shape=(
                 jax.ShapeDtypeStruct((MATS,) + block, F32),
                 jax.ShapeDtypeStruct((MATS,) + block, F32),
                 jax.ShapeDtypeStruct((HEAD, 4) + block, BF16),
-                jax.ShapeDtypeStruct((TAIL_A,) + block, BF16),
-                jax.ShapeDtypeStruct((TAIL_B,) + block, BF16),
-            ),
+            )
+            + tuple(jax.ShapeDtypeStruct((n,) + block, BF16) for n in TAILS),
             in_specs=[hbm, hbm, hbm, smem, smem],
-            out_specs=[hbm] * 5,
+            out_specs=[hbm] * (3 + len(TAILS)),
             scratch_shapes=[
                 pltpu.VMEM((2, 2) + block, F32),
                 pltpu.VMEM((A_SLOTS, 2) + block, F32),
@@ -520,6 +568,7 @@
                 pltpu.VMEM((MATS,) + block, BF16),
                 pltpu.VMEM((COLS, COLS), BF16),
                 pltpu.VMEM((COLS, COLS), BF16),
+                dma((PIECES + 1,)), dma((PIECES + 1,)),
                 dma((2,)), dma((A_SLOTS,)), dma((A_SLOTS,)), dma((LAG,)), dma((B_SLOTS,)),
                 dma((2,)), dma((2,)), dma((2,)), dma((2,)),
                 dma((DEVS,)), dma((MATS,)), dma((MATS,)), dma((MATS,)),
@@ -545,16 +594,13 @@
         def move(value, pairs):
             return lax.ppermute(value, "dp", pairs)
 
-        nbr_a = move(tail_a, across)
-        nbr_b = move(tail_b, across)
-        par_a = move(tail_a, beside)
-        par_b = move(tail_b, beside)
-        fwd_a = move(nbr_a, beside)
-        fwd_b = move(nbr_b, beside)
+        nbr = [move(part, across) for part in tails]
+        par = [move(part, beside) for part in tails]
+        fwd = [move(part, beside) for part in nbr]
         mom_new, weight_new, full = publish(mom_new, weight_new, head)
         full = full.reshape((MATS, 4) + block)
-        full = fill(full, HEAD, tail_a, par_a, nbr_a, fwd_a)
-        full = fill(full, HEAD + TAIL_A, tail_b, par_b, nbr_b, fwd_b)
+        for n, part in enumerate(tails):
+            full = fill(full, HEAD + sum(TAILS[:n]), part, par[n], nbr[n], fwd[n])
         return (
             mom_new.reshape((MATS,) + block),
             weight_new.reshape((MATS,) + block),

time: 884 us -> 872 us (0.986)
  waiting for transfers between devices: 68.1 us -> 58.7 us
    ppermute x6 -> x9, waiting for transfers between devices: 68.1 us -> 58.7 us  [move(): return lax.ppermute(value, 'dp', pairs)]
  transfers between devices with their start and end apart: 6 -> 9, of which waited for: 1 -> 1; matrix products, arithmetic and copies ran while one was open for 0% -> 0% of each run, Pallas kernels for 6% -> 6%
where the time goes in v3:
time: 872 us
  Pallas kernels  807 us (93%)
  waiting for transfers between devices  58.7 us (7%)
    pallas_call x1, Pallas kernels, local_step(): pl.pallas_call(kernel, name='muon_step', out_shape=(jax.ShapeDtypeStruct(...  753 us
    ppermute x9, waiting for transfers between devices, move(): return lax.ppermute(value, 'dp', pairs)  58.7 us
    pallas_call x1, Pallas kernels, publish(): pl.pallas_call(publish_kernel, name='publish', grid=(steps,), out_shape=(...  43.2 us
  transfers between devices with their start and end apart: 9, of which 1 were waited for; matrix products, arithmetic and copies ran while one was open for 0% of the time, Pallas kernels for 6%

profile of v3, /device:TPU:0, one launch (start us, length us, event | category | flops | bytes accessed | tf_op | source)
XLA Modules:
  0.0 872.2 jit_solution(10496333579174752834)
XLA Ops:
  1.3 752.6 %muon_step.1 = (f32[24,512,384]{2,1,0:T(8,128)}, f32[24,512,384]{2,1,0:T(8,128)}, bf16[16,4,512,384]{3,2,1,0:T(8,128)(2,1)}, bf16[5,512,384]{2,1,0:T(8,128)(2,1)...) custom-call(f32[24,2,2,512,384]{4,3,2,1,0:T(8,128)} %bitcast.grad, f32[24,512,384]{2,1,0:T(8,128)} %mom.1, ...), custom_call_target="tpu_custom_call" | custom-call | flops 86100000768 | bytes 400000000 | tf_op jit(solution)/shard_map/muon_step/pallas_call | solution.py:544
  753.9 1.5 collective-permute-start.7
  755.4 0.5 collective-permute-start.4
  756.0 0.0 collective-permute-start.6
  756.0 0.5 collective-permute-start.3
  756.5 1.5 collective-permute-start.1
  758.0 58.7 %collective-permute-done.4.nbr = bf16[2,512,384]{2,1,0:T(8,128)(2,1)S(1)} collective-permute-done((bf16[2,512,384]{2,1,0:T(8,128)(2,1)}, bf16[2,512,384]{2,1,0:T(8,128)(2,1)S(1)}, u32[]{:S(2)}, u32[]{:S(2)}) %collective-permute-start.4) | collective-permute-done | bytes 786464 | tf_op jit(solution)/shard_map/ppermute | solution.py:595
  816.7 0.0 collective-permute-start.5
  816.7 0.0 collective-permute-done.7.nbr
  816.7 0.5 collective-permute-start.8
  817.2 0.0 copy-start
  817.2 43.2 %publish.1 = (f32[12288,384]{1,0:T(8,128)}, f32[12288,384]{1,0:T(8,128)}, bf16[49152,384]{1,0:T(8,128)(2,1)}) custom-call(f32[12288,384]{1,0:T(8,128)} %bitcast.15, f32[12288,384]{1,0:T(8,128)} %bitcast.16, bf16[32768,384]{1,0:T(8,128)(2,1)} %bitcast.12), custom_call_target="tpu_custom_call" | custom-call | flops 40000000000 | bytes 126000000 | tf_op jit(solution)/shard_map/publish/pallas_call | solution.py:489
  860.5 0.0 collective-permute-done.1.nbr
  860.5 0.0 collective-permute-start
  860.5 0.0 collective-permute-done.6.par
  860.5 0.5 collective-permute-start.2
  861.0 0.0 collective-permute-done.8.fwd
  861.0 0.0 copy-done
  861.0 0.0 copy-start.1
  861.0 6.1 fill.3.whole
  867.1 0.0 copy-start.2
  867.1 0.0 collective-permute-done.3.par
  867.1 0.0 collective-permute-done.5.fwd
  867.1 0.0 copy-done.1
  867.1 2.9 fill.4.whole
  870.0 0.0 collective-permute-done.par
  870.0 0.0 collective-permute-done.2.fwd
  870.0 0.0 copy-done.2
  870.1 2.2 fill.5
Async XLA Ops:
  753.9 62.8 %collective-permute-start.7 = (bf16[5,512,384]{2,1,0:T(8,128)(2,1)}, bf16[5,512,384]{2,1,0:T(8,128)(2,1)}, u32[]{:S(2)}, u32[]{:S(2)}) collective-permute-start(bf16[5,512,384]{2,1,0:T(8,128)(2,1)} %get-tuple-element.19.own), channel_id=1, source_target_pairs={{0,2},{1,3},{2,0},{3,1},{4,6},{5,7},{6,4},{7,5}} | collective-permute-start | bytes 5898248 | tf_op jit(solution)/shard_map/ppermute | solution.py:595
  755.4 61.2 %collective-permute-start.4 = (bf16[2,512,384]{2,1,0:T(8,128)(2,1)}, bf16[2,512,384]{2,1,0:T(8,128)(2,1)S(1)}, u32[]{:S(2)}, u32[]{:S(2)}) collective-permute-start(bf16[2,512,384]{2,1,0:T(8,128)(2,1)} %get-tuple-element.18.own), channel_id=1, source_target_pairs={{0,2},{1,3},{2,0},{3,1},{4,6},{5,7},{6,4},{7,5}} | collective-permute-start | bytes 2359304 | tf_op jit(solution)/shard_map/ppermute | solution.py:595
  756.0 104.5 %collective-permute-start.6 = (bf16[5,512,384]{2,1,0:T(8,128)(2,1)}, bf16[5,512,384]{2,1,0:T(8,128)(2,1)}, u32[]{:S(2)}, u32[]{:S(2)}) collective-permute-start(bf16[5,512,384]{2,1,0:T(8,128)(2,1)} %get-tuple-element.19.own), channel_id=1, source_target_pairs={{0,1},{1,0},{2,3},{3,2},{4,5},{5,4},{6,7},{7,6}} | collective-permute-start | bytes 5898248 | tf_op jit(solution)/shard_map/ppermute | solution.py:595
  756.0 111.1 %collective-permute-start.3 = (bf16[2,512,384]{2,1,0:T(8,128)(2,1)}, bf16[2,512,384]{2,1,0:T(8,128)(2,1)S(1)}, u32[]{:S(2)}, u32[]{:S(2)}) collective-permute-start(bf16[2,512,384]{2,1,0:T(8,128)(2,1)} %get-tuple-element.18.own), channel_id=1, source_target_pairs={{0,1},{1,0},{2,3},{3,2},{4,5},{5,4},{6,7},{7,6}} | collective-permute-start | bytes 2359304 | tf_op jit(solution)/shard_map/ppermute | solution.py:595
  756.5 104.0 %collective-permute-start.1 = (bf16[1,512,384]{2,1,0:T(8,128)(2,1)}, bf16[1,512,384]{2,1,0:T(8,128)(2,1)}, u32[]{:S(2)}, u32[]{:S(2)}) collective-permute-start(bf16[1,512,384]{2,1,0:T(8,128)(2,1)} %get-tuple-element.17.own), channel_id=1, source_target_pairs={{0,2},{1,3},{2,0},{3,1},{4,6},{5,7},{6,4},{7,5}} | collective-permute-start | bytes 1179656 | tf_op jit(solution)/shard_map/ppermute | solution.py:595
  816.7 50.4 %collective-permute-start.5 = (bf16[2,512,384]{2,1,0:T(8,128)(2,1)S(1)}, bf16[2,512,384]{2,1,0:T(8,128)(2,1)}, u32[]{:S(2)}, u32[]{:S(2)}) collective-permute-start(bf16[2,512,384]{2,1,0:T(8,128)(2,1)S(1)} %collective-permute-done.4.nbr), channel_id=1, source_target_pairs={{0,1},{1,0},{2,3},{3,2},{4,5},{5,4},{6,7},{7,6}} | collective-permute-start | bytes 2359304 | tf_op jit(solution)/shard_map/ppermute | solution.py:595
  816.7 44.3 %collective-permute-start.8 = (bf16[5,512,384]{2,1,0:T(8,128)(2,1)}, bf16[5,512,384]{2,1,0:T(8,128)(2,1)}, u32[]{:S(2)}, u32[]{:S(2)}) collective-permute-start(bf16[5,512,384]{2,1,0:T(8,128)(2,1)} %collective-permute-done.7.nbr), channel_id=1, source_target_pairs={{0,1},{1,0},{2,3},{3,2},{4,5},{5,4},{6,7},{7,6}} | collective-permute-start | bytes 5898248 | tf_op jit(solution)/shard_map/ppermute | solution.py:595
  817.2 43.8 %copy-start = (bf16[5,512,384]{2,1,0:T(8,128)(2,1)S(1)}, bf16[5,512,384]{2,1,0:T(8,128)(2,1)}, u32[]{:S(2)}) copy-start(bf16[5,512,384]{2,1,0:T(8,128)(2,1)} %get-tuple-element.19.own) | copy-start | bytes 5898244
  860.5 9.6 %collective-permute-start = (bf16[1,512,384]{2,1,0:T(8,128)(2,1)}, bf16[1,512,384]{2,1,0:T(8,128)(2,1)S(1)}, u32[]{:S(2)}, u32[]{:S(2)}) collective-permute-start(bf16[1,512,384]{2,1,0:T(8,128)(2,1)} %get-tuple-element.17.own), channel_id=1, source_target_pairs={{0,1},{1,0},{2,3},{3,2},{4,5},{5,4},{6,7},{7,6}} | collective-permute-start | bytes 1179656 | tf_op jit(solution)/shard_map/ppermute | solution.py:595
  860.5 9.6 %collective-permute-start.2 = (bf16[1,512,384]{2,1,0:T(8,128)(2,1)}, bf16[1,512,384]{2,1,0:T(8,128)(2,1)S(1)}, u32[]{:S(2)}, u32[]{:S(2)}) collective-permute-start(bf16[1,512,384]{2,1,0:T(8,128)(2,1)} %collective-permute-done.1.nbr), channel_id=1, source_target_pairs={{0,1},{1,0},{2,3},{3,2},{4,5},{5,4},{6,7},{7,6}} | collective-permute-start | bytes 1179656 | tf_op jit(solution)/shard_map/ppermute | solution.py:595
  861.0 6.1 copy-start.1
  867.1 3.0 copy-start.2
